TPU v7x, 32 devices: a whole 2x2x4 slice. The times are simulated.
32 devices in a mesh: dp: 8 (over z, core), tensor: 4 (over y, x).
Axes of the slice: x: 2, y: 2, z: 4, core: 2. Of those that a mesh axis runs over, the one named last changes fastest.
Arguments:
- tokens: bfloat16 [10240, 4096], P(('dp', 'tensor')), parts along dimension 0, may hold values from -6 to 6
- norm_gain: bfloat16 [4096], replicated, may hold values from 0.099609375 to 1.8984375
- query_weight: bfloat16 [4096, 8192], P(None, 'tensor'), may hold values from -0.09375 to 0.09375
- key_weight: bfloat16 [4096, 1024], P(None, 'tensor'), may hold values from -0.09375 to 0.09375
- value_weight: bfloat16 [4096, 1024], P(None, 'tensor'), may hold values from -0.09375 to 0.09375
- out_weight: bfloat16 [8192, 4096], P('tensor'), may hold values from -0.0625 to 0.0625
- past_cache: bfloat16 [1024, 64, 2, 1024], P('dp', None, None, 'tensor'), parts along dimension 0, may hold values from -320 to 320
- exponents: int32 [10240, 32], P('dp'), parts along dimension 0, may hold values from -11 to -7
Outputs:
- mixed: bfloat16 [10240, 4096], P(('dp', 'tensor')), parts along dimension 0
There are 8 independent parts, one for each index of `dp`. A program takes and returns all parts, laid end to end along the dimension named above; an argument that names none is the same for every part. Nothing has to cross between parts.
All inputs are finite; a program needn't handle non-finite values.
Results may differ from a plain program's by a relative error of at most 0.012.
The roundings to bfloat16 on the way count: a program that leaves them out, or rounds other values in their place, can miss the bound.
Values may be sent and summed in bfloat16 or wider, within the bound.
A program may use at most 192 MiB of HBM per device.

v0:
```python
import functools

import jax
import jax.numpy as jnp
from jax import lax
from jax.experimental import pallas as pl
from jax.experimental.pallas import tpu as pltpu
from jax.sharding import PartitionSpec as P

HD = 128
NEW = 10
CHUNKS = 2
SEQ_BLOCK = 8

epsilon = 1e-05
theta_base = 500000.0


def rotary_tables(row_count):
    half_dim = HD // 2
    positions = (jnp.arange(row_count, dtype=jnp.int32) % NEW + 64).astype(jnp.float32)
    frequency = theta_base ** (-(jnp.arange(half_dim, dtype=jnp.float32) * 2.0) / HD)
    angles = positions[:, None] * frequency[None, :]
    cosine = jnp.cos(angles)
    sine_part = jnp.sin(angles)
    return (
        jnp.concatenate([cosine, cosine], 1),
        jnp.concatenate([-sine_part, sine_part], 1),
    )


def turn(block, cosine, sine_part):
    heads = []
    for h in range(block.shape[1] // HD):
        head = block[:, h * HD : (h + 1) * HD]
        heads.append(head * cosine + pltpu.roll(head, HD // 2, 1) * sine_part)
    return jnp.concatenate(heads, 1) if len(heads) > 1 else heads[0]


def project_kernel(x_ref, wq_ref, wk_ref, wv_ref, cos_ref, sin_ref, q_ref, k_ref, v_ref):
    normed = x_ref[...]
    cosine = cos_ref[...]
    sine_part = sin_ref[...]

    @pl.when(pl.program_id(0) == 0)
    def _():
        key = jnp.dot(normed, wk_ref[...], preferred_element_type=jnp.float32)
        k_ref[...] = turn(key, cosine, sine_part).astype(jnp.bfloat16)
        value = jnp.dot(normed, wv_ref[...], preferred_element_type=jnp.float32)
        v_ref[...] = value.astype(jnp.bfloat16)

    query = jnp.dot(normed, wq_ref[...], preferred_element_type=jnp.float32)
    q_ref[...] = turn(query, cosine, sine_part).astype(jnp.bfloat16)


def project(normed, query_weight, key_weight, value_weight, cosine, sine_part):
    rows, depth = normed.shape
    q_cols = query_weight.shape[1]
    k_cols = key_weight.shape[1]
    width = 512
    whole = lambda j: (0, 0)
    return pl.pallas_call(
        project_kernel,
        grid=(q_cols // width,),
        in_specs=[
            pl.BlockSpec((rows, depth), whole),
            pl.BlockSpec((depth, width), lambda j: (0, j)),
            pl.BlockSpec((depth, k_cols), whole),
            pl.BlockSpec((depth, k_cols), whole),
            pl.BlockSpec((rows, HD), whole),
            pl.BlockSpec((rows, HD), whole),
        ],
        out_specs=[
            pl.BlockSpec((rows, width), lambda j: (0, j)),
            pl.BlockSpec((rows, k_cols), whole),
            pl.BlockSpec((rows, k_cols), whole),
        ],
        out_shape=[
            jax.ShapeDtypeStruct((rows, q_cols), jnp.bfloat16),
            jax.ShapeDtypeStruct((rows, k_cols), jnp.bfloat16),
            jax.ShapeDtypeStruct((rows, k_cols), jnp.bfloat16),
        ],
        compiler_params=pltpu.CompilerParams(vmem_limit_bytes=56 * 1024 * 1024),
    )(normed, query_weight, key_weight, value_weight, cosine, sine_part)


def attend_kernel(kv_heads, group, q_ref, k_ref, v_ref, cache_ref, bias_ref, out_ref):
    rows = q_ref.shape[0]
    inv_root = 1.0 / HD**0.5
    bias = bias_ref[...]
    for kv in range(kv_heads):
        base = kv * group * HD
        query = jnp.concatenate(
            [q_ref[:, base + g * HD : base + (g + 1) * HD] for g in range(group)], 0
        )
        span = slice(kv * HD, (kv + 1) * HD)
        v_span = slice((kv_heads + kv) * HD, (kv_heads + kv + 1) * HD)
        keys = jnp.concatenate([cache_ref[:, span], k_ref[:, span]], 0)
        values = jnp.concatenate([cache_ref[:, v_span], v_ref[:, span]], 0)
        scores = lax.dot_general(
            query, keys, (((1,), (1,)), ((), ())), preferred_element_type=jnp.float32
        )
        weights = []
        for g in range(group):
            part = scores[g * rows : (g + 1) * rows] * inv_root + bias
            probs = jnp.exp(part - jnp.max(part, axis=-1, keepdims=True))
            scale = 1.0 / jnp.sum(probs, axis=-1, keepdims=True)
            weights.append((probs * scale).astype(jnp.bfloat16))
        combined = jnp.dot(
            jnp.concatenate(weights, 0), values, preferred_element_type=jnp.float32
        ).astype(jnp.bfloat16)
        for g in range(group):
            out_ref[:, base + g * HD : base + (g + 1) * HD] = combined[
                g * rows : (g + 1) * rows
            ]


def attend(query, key_new, value_new, cache, cache_len, ranks, chunk):
    rows, q_cols = query.shape
    k_cols = key_new.shape[1]
    kv_heads = k_cols // HD
    group = q_cols // k_cols
    block_rows = SEQ_BLOCK * NEW
    blocks = rows // block_rows
    per_rank = blocks // ranks
    cache_rows = SEQ_BLOCK * cache_len
    row_seq = jnp.arange(block_rows)[:, None] // NEW
    row_new = jnp.arange(block_rows)[:, None] % NEW
    in_cache = row_seq == jnp.arange(cache_rows)[None, :] // cache_len
    new_col = jnp.arange(block_rows)[None, :]
    in_new = (row_seq == new_col // NEW) & (row_new >= new_col % NEW)
    bias = jnp.where(jnp.concatenate([in_cache, in_new], 1), 0.0, -1e30).astype(jnp.float32)
    return pl.pallas_call(
        functools.partial(attend_kernel, kv_heads, group),
        grid=(blocks,),
        in_specs=[
            pl.BlockSpec((block_rows, q_cols), lambda i: (i, 0)),
            pl.BlockSpec((block_rows, k_cols), lambda i: (i, 0)),
            pl.BlockSpec((block_rows, k_cols), lambda i: (i, 0)),
            pl.BlockSpec(
                (cache_rows, 2 * k_cols),
                lambda i: (
                    (i // per_rank) * (per_rank * CHUNKS) + chunk * per_rank + i % per_rank,
                    0,
                ),
            ),
            pl.BlockSpec((block_rows, cache_rows + block_rows), lambda i: (0, 0)),
        ],
        out_specs=pl.BlockSpec((block_rows, q_cols), lambda i: (i, 0)),
        out_shape=jax.ShapeDtypeStruct((rows, q_cols), jnp.bfloat16),
        compiler_params=pltpu.CompilerParams(vmem_limit_bytes=56 * 1024 * 1024),
    )(query, key_new, value_new, cache, bias)


def out_kernel(group_cols, a_ref, w_ref, shrink_ref, out_ref):
    partial_value = jnp.dot(a_ref[...], w_ref[...], preferred_element_type=jnp.float32)
    for i in range(out_ref.shape[1] // group_cols):
        span = slice(i * group_cols, (i + 1) * group_cols)
        scaled = jnp.clip(partial_value[:, span] * shrink_ref[0, :, i : i + 1], -127.0, 127.0)
        out_ref[:, span] = scaled.astype(jnp.bfloat16)


def project_out(attended, out_weight, shrink):
    rows, depth = attended.shape
    cols = out_weight.shape[1]
    groups = shrink.shape[1]
    group_cols = cols // groups
    width = 512
    per_block = width // group_cols
    shrink = shrink.reshape(rows, groups // per_block, per_block).transpose(1, 0, 2)
    return pl.pallas_call(
        functools.partial(out_kernel, group_cols),
        grid=(cols // width,),
        in_specs=[
            pl.BlockSpec((rows, depth), lambda j: (0, 0)),
            pl.BlockSpec((depth, width), lambda j: (0, j)),
            pl.BlockSpec((1, rows, per_block), lambda j: (j, 0, 0)),
        ],
        out_specs=pl.BlockSpec((rows, width), lambda j: (0, j)),
        out_shape=jax.ShapeDtypeStruct((rows, cols), jnp.bfloat16),
        compiler_params=pltpu.CompilerParams(vmem_limit_bytes=56 * 1024 * 1024),
    )(attended, out_weight, shrink)


def norm_kernel(x_ref, gain_ref, out_ref):
    floats = x_ref[...].astype(jnp.float32)
    normed = floats * lax.rsqrt(jnp.mean(floats * floats, axis=-1, keepdims=True) + epsilon)
    out_ref[...] = (normed * gain_ref[...].astype(jnp.float32)).astype(jnp.bfloat16)


def normalise(tokens, gain, step, chunk):
    depth = tokens.shape[1]
    return pl.pallas_call(
        norm_kernel,
        grid=(1,),
        in_specs=[
            pl.BlockSpec((step, depth), lambda i: (chunk, 0)),
            pl.BlockSpec((1, depth), lambda i: (0, 0)),
        ],
        out_specs=pl.BlockSpec((step, depth), lambda i: (0, 0)),
        out_shape=jax.ShapeDtypeStruct((step, depth), jnp.bfloat16),
    )(tokens, gain)


def residual_kernel(tokens_ref, restore_ref, *refs):
    out_ref = refs[-1]
    start = 0
    groups = restore_ref.shape[1]
    width = tokens_ref.shape[1] // groups
    for share_ref in refs[:-1]:
        rows = slice(start, start + share_ref.shape[0])
        start += share_ref.shape[0]
        for g in range(groups):
            cols = slice(g * width, (g + 1) * width)
            term = share_ref[:, cols].astype(jnp.float32) * restore_ref[rows, g : g + 1]
            out_ref[rows, cols] = (tokens_ref[rows, cols].astype(jnp.float32) + term).astype(
                jnp.bfloat16
            )


def add_residual(tokens, shares, restore):
    return pl.pallas_call(
        residual_kernel,
        out_shape=jax.ShapeDtypeStruct(tokens.shape, jnp.bfloat16),
    )(tokens, restore, *shares)


def on_device(
    tokens, norm_gain, query_weight, key_weight, value_weight, out_weight, past_cache, exponents
):
    own_rows, depth = tokens.shape
    ranks = lax.axis_size("tensor")
    step = own_rows // CHUNKS
    groups = exponents.shape[1]
    cache_len = past_cache.shape[1]
    gathered = []
    for c in range(CHUNKS):
        normed = normalise(tokens, norm_gain.reshape(1, depth), step, c)
        gathered.append(lax.all_gather(normed, "tensor", axis=0, tiled=True))
    cache = past_cache.reshape(past_cache.shape[0] * cache_len, -1)
    cosine, sine_part = rotary_tables(step * ranks)
    shrink = jnp.exp2(-exponents.astype(jnp.float32)).reshape(ranks, CHUNKS, step, groups)
    shares = []
    for c in range(CHUNKS):
        query, key_new, value_new = project(
            gathered[c], query_weight, key_weight, value_weight, cosine, sine_part
        )
        attended = attend(query, key_new, value_new, cache, cache_len, ranks, c)
        rounded = project_out(
            attended, out_weight, shrink[:, c].reshape(ranks * step, groups)
        )
        shares.append(lax.psum_scatter(rounded, "tensor", scatter_dimension=0, tiled=True))
    own_exponents = lax.dynamic_slice_in_dim(
        exponents, lax.axis_index("tensor") * own_rows, own_rows, 0
    )
    restore = jnp.exp2(own_exponents.astype(jnp.float32))
    return add_residual(tokens, shares, restore)


def solution(mesh):
    return jax.shard_map(
        on_device,
        mesh=mesh,
        in_specs=(
            P(("dp", "tensor"), None),
            P(),
            P(None, "tensor"),
            P(None, "tensor"),
            P(None, "tensor"),
            P("tensor", None),
            P("dp", None, None, "tensor"),
            P("dp", None),
        ),
        out_specs=P(("dp", "tensor"), None),
        check_vma=False,
    )
```

profile of v0, /device:TPU:0, one launch (start us, length us, event | category | flops | bytes accessed | tf_op | source)
XLA Modules:
  0.0 279.0 jit_solution(15868129733131798306)
XLA Ops:
  6.5 1.3 reshape.135.gain_ref
  7.8 3.1 %shard_map.86 = bf16[160,4096]{1,0:T(8,128)(2,1)} custom-call(bf16[320,4096]{1,0:T(8,128)(2,1)} %tokens_ref.1, bf16[1,4096]{1,0:T(2,128)(2,1)} %reshape.135.gain_ref), custom_call_target="tpu_custom_call" | custom-call | tf_op jit(solution)/shard_map/pallas_call | solution.py:193
  11.0 3.2 %shard_map.82 = bf16[160,4096]{1,0:T(8,128)(2,1)} custom-call(bf16[320,4096]{1,0:T(8,128)(2,1)} %tokens_ref.1, bf16[1,4096]{1,0:T(2,128)(2,1)} %reshape.135.gain_ref), custom_call_target="tpu_custom_call" | custom-call | tf_op jit(solution)/shard_map/pallas_call | solution.py:193
  14.3 8.7 %copy.18 = bf16[1024,8,2,256]{3,1,2,0:T(8,128)(2,1)} copy(bf16[1024,8,2,256]{3,2,1,0:T(2,128)(2,1)} %bitcast.15) | data formatting | bytes 16777216
  23.0 0.4 reshape.137
  23.4 0.8 slice_reduce_fusion
  24.3 2.3 copy.14
  26.8 0.7 add_select_fusion.bias_ref
  27.5 1.2 fusion
  28.7 1.2 pad_maximum_fusion
  29.9 45.2 %all-gather.5.cloned.1.call-done.x_ref = bf16[640,4096]{1,0:T(8,128)(2,1)} async-done(((bf16[160,4096]{1,0:T(8,128)(2,1)}), bf16[640,4096]{1,0:T(8,128)(2,1)}) %all-gather.5.cloned.1.call-update) | async-done | bytes 5242896 | tf_op jit(solution)/shard_map/all_gather | solution.py:239
  75.2 23.0 %shard_map.87 = (bf16[640,2048]{1,0:T(8,128)(2,1)}, bf16[640,256]{1,0:T(8,128)(2,1)}, bf16[640,256]{1,0:T(8,128)(2,1)}) custom-call(bf16[640,4096]{1,0:T(8,128)(2,1)} %all-gather.5.cloned.1.call-done.x_ref, bf16[4096,2048]{1,0:T(8,128)(2,1)} %wq_ref.3, bf16[4096,256]{1,0:T(8,128)(2,1)} %wk_ref.3, bf16[4096,256]{1,0:T(8,128)(2,1)} %wv_ref.3, ...), custom_call_target="tpu_custom_call" | custom-call | tf_op jit(solution)/shard_map/pallas_call | solution.py:62
  98.1 19.4 %shard_map.88.a_ref = bf16[640,2048]{1,0:T(8,128)(2,1)} custom-call(bf16[640,2048]{1,0:T(8,128)(2,1)} %get-tuple-element.14.q_ref, bf16[640,256]{1,0:T(8,128)(2,1)} %get-tuple-element.15.k_ref, bf16[640,256]{1,0:T(8,128)(2,1)} %get-tuple-element.16.v_ref, bf16[8192,512]{1,0:T(8,128)(2,1)} %bitcast.11, f32[80,592]{1,0:T(8,128)} %add_select_fusion.bias_ref), custom_call_target="tpu_custom_call" | custom-call | tf_op jit(solution)/shard_map/pallas_call | solution.py:133
  117.5 16.9 %shard_map.89 = bf16[640,4096]{1,0:T(8,128)(2,1)} custom-call(bf16[640,2048]{1,0:T(8,128)(2,1)} %shard_map.88.a_ref, bf16[2048,4096]{1,0:T(8,128)(2,1)} %w_ref.3, f32[8,640,4]{2,1,0:T(8,128)} %bitcast.13), custom_call_target="tpu_custom_call" | custom-call | tf_op jit(solution)/shard_map/pallas_call | solution.py:171
  134.4 0.2 reduce-scatter.3.cloned.1.call-start
  134.8 2.3 copy.12
  137.1 1.3 all-gather.3.cloned.1.call-done.x_ref
  138.3 23.0 %shard_map.83 = (bf16[640,2048]{1,0:T(8,128)(2,1)}, bf16[640,256]{1,0:T(8,128)(2,1)}, bf16[640,256]{1,0:T(8,128)(2,1)}) custom-call(bf16[640,4096]{1,0:T(8,128)(2,1)} %all-gather.3.cloned.1.call-done.x_ref, bf16[4096,2048]{1,0:T(8,128)(2,1)} %wq_ref.3, bf16[4096,256]{1,0:T(8,128)(2,1)} %wk_ref.3, bf16[4096,256]{1,0:T(8,128)(2,1)} %wv_ref.3, ...), custom_call_target="tpu_custom_call" | custom-call | tf_op jit(solution)/shard_map/pallas_call | solution.py:62
  161.3 19.4 %shard_map.84.a_ref = bf16[640,2048]{1,0:T(8,128)(2,1)} custom-call(bf16[640,2048]{1,0:T(8,128)(2,1)} %get-tuple-element.11.q_ref, bf16[640,256]{1,0:T(8,128)(2,1)} %get-tuple-element.12.k_ref, bf16[640,256]{1,0:T(8,128)(2,1)} %get-tuple-element.13.v_ref, bf16[8192,512]{1,0:T(8,128)(2,1)} %bitcast.12, f32[80,592]{1,0:T(8,128)} %add_select_fusion.bias_ref), custom_call_target="tpu_custom_call" | custom-call | tf_op jit(solution)/shard_map/pallas_call | solution.py:133
  180.7 17.0 %shard_map.85 = bf16[640,4096]{1,0:T(8,128)(2,1)} custom-call(bf16[640,2048]{1,0:T(8,128)(2,1)} %shard_map.84.a_ref, bf16[2048,4096]{1,0:T(8,128)(2,1)} %w_ref.3, f32[8,640,4]{2,1,0:T(8,128)} %bitcast.14), custom_call_target="tpu_custom_call" | custom-call | tf_op jit(solution)/shard_map/pallas_call | solution.py:171
  197.9 0.7 multiply_exponential_fusion.1.restore_ref
  198.6 4.0 %reduce-scatter.5.cloned.1.call-done.refs_1_ = bf16[160,4096]{1,0:T(8,128)(2,1)} async-done(((bf16[640,4096]{1,0:T(8,128)(2,1)}), bf16[160,4096]{1,0:T(8,128)(2,1)}) %reduce-scatter.5.cloned.1.call-update) | async-done | bytes 1310736 | tf_op jit(solution)/shard_map/reduce_scatter | solution.py:252
  202.7 64.2 %reduce-scatter.3.cloned.1.call-done.refs_0_ = bf16[160,4096]{1,0:T(8,128)(2,1)} async-done(((bf16[640,4096]{1,0:T(8,128)(2,1)}), bf16[160,4096]{1,0:T(8,128)(2,1)}) %reduce-scatter.3.cloned.1.call-update) | async-done | bytes 1310736 | tf_op jit(solution)/shard_map/reduce_scatter | solution.py:252
  266.9 5.6 %shard_map.90 = bf16[320,4096]{1,0:T(8,128)(2,1)} custom-call(bf16[320,4096]{1,0:T(8,128)(2,1)} %tokens_ref.1, f32[320,32]{1,0:T(8,128)} %multiply_exponential_fusion.1.restore_ref, bf16[160,4096]{1,0:T(8,128)(2,1)} %reduce-scatter.3.cloned.1.call-done.refs_0_, bf16[160,4096]{1,0:T(8,128)(2,1)} %reduce-scatter.5.cloned.1.call-done.refs_1_), custom_call_target="tpu_custom_call" | custom-call | tf_op jit(solution)/shard_map/pallas_call | solution.py:222
  (20 shorter events, 0.9 us)
Async XLA Ops:
  6.5 68.6 %all-gather.5.cloned.1.call-start = ((), (), s32[]{:S(2)}) async-start(), calls=%async_computation.4 | async-start | bytes 6553600 | tf_op jit(solution)/shard_map/all_gather | solution.py:239
  11.0 127.4 %all-gather.3.cloned.1.call-start = ((), (), s32[]{:S(2)}) async-start(), calls=%async_computation.2 | async-start | bytes 6553600 | tf_op jit(solution)/shard_map/all_gather | solution.py:239
  14.2 188.4 %reduce-scatter.5.cloned.1.call-start = ((), (), s32[]{:S(2)}) async-start(), calls=%async_computation.5 | async-start | bytes 6553600 | tf_op jit(solution)/shard_map/reduce_scatter | solution.py:252
  14.3 8.7 %copy-start = (s32[1280,32]{0,1:T(8,128)S(1)}, s32[1280,32]{0,1:T(8,128)}, u32[]{:S(2)}) copy-start(s32[1280,32]{0,1:T(8,128)} %param.15) | copy-start | bytes 491524
  134.4 132.5 %reduce-scatter.3.cloned.1.call-start = ((), (), s32[]{:S(2)}) async-start(), calls=%async_computation.3 | async-start | bytes 6553600 | tf_op jit(solution)/shard_map/reduce_scatter | solution.py:252
Sparse Core Ops, SparseCore 0:
  11.1 64.0 all-gather.4
  77.0 61.2 all-gather.2
  141.3 61.3 reduce-scatter.4
  205.5 61.3 reduce-scatter.2
where the time goes:
time: 280 us; the launch traced here: 279 us
  Pallas kernels  131 us (47%)
  waiting for transfers between devices  115 us (41%)
  local copies, waits for them, and re-layouts  16.2 us (6%)
  between operations  13.2 us (5%)
  other arithmetic  4.02 us (1%)
    reduce_scatter x2, waiting for transfers between devices, on_device(): lax.psum_scatter(rounded, 'tensor', scatter_dimension=0, tiled=True)  68.2 us
    all_gather x2, waiting for transfers between devices, on_device(): gathered.append(lax.all_gather(normed, 'tensor', axis=0, tiled=True))  46.5 us
    pallas_call x2, Pallas kernels, project(): pl.pallas_call(project_kernel, grid=(q_cols // width,), in_specs=[pl.Bloc...  46 us
    pallas_call x2, Pallas kernels, attend(): pl.pallas_call(functools.partial(attend_kernel, kv_heads, group), grid=(b...  38.7 us
    pallas_call x2, Pallas kernels, project_out(): pl.pallas_call(functools.partial(out_kernel, group_cols), grid=(cols // w...  33.9 us
    unnamed x4, local copies, waits for them, and re-layouts  8.77 us
    pallas_call x2, Pallas kernels, normalise(): pl.pallas_call(norm_kernel, grid=(1,), in_specs=[pl.BlockSpec((step, dept...  6.3 us
    pallas_call x1, Pallas kernels, add_residual(): pl.pallas_call(residual_kernel, out_shape=jax.ShapeDtypeStruct(tokens.sha...  5.61 us
  transfers between devices with their start and end apart: 4, of which 4 were waited for; matrix products, arithmetic and copies ran while one was open for 7% of the time, Pallas kernels for 44%

commit v1 on v0

v1 whole, which is shorter than its diff:
```python
import functools

import jax
import jax.numpy as jnp
import numpy as np
from jax import lax
from jax.experimental import pallas as pl
from jax.experimental.pallas import tpu as pltpu
from jax.sharding import PartitionSpec as P

HD = 128
NEW = 10
SEQ_BLOCK = 8
PIECE = SEQ_BLOCK * NEW
WIDTH = 512

epsilon = 1e-05
theta_base = 500000.0
MESH = pl.DeviceIdType.MESH


def rotary_tables(cache_len):
    half_dim = HD // 2
    positions = np.arange(PIECE) % NEW + cache_len
    frequency = theta_base ** (-(np.arange(half_dim) * 2.0) / HD)
    angles = positions[:, None] * frequency[None, :]
    cosine = np.cos(angles)
    sine_part = np.sin(angles)
    return (
        np.concatenate([cosine, cosine], 1).astype(np.float32),
        np.concatenate([-sine_part, sine_part], 1).astype(np.float32),
    )


def mask_table(cache_len):
    row = np.arange(PIECE)[:, None]
    cached = np.arange(SEQ_BLOCK * cache_len)[None, :]
    fresh = np.arange(PIECE)[None, :]
    in_cache = row // NEW == cached // cache_len
    in_new = (row // NEW == fresh // NEW) & (row % NEW >= fresh % NEW)
    return np.where(np.concatenate([in_cache, in_new], 1), 0.0, -1e30).astype(np.float32)


def ring_index(place, ranks):
    half = ranks // 2
    return jnp.where(place < half, place, half + ranks - 1 - place)


def layer_kernel(
    ranks,
    batches,
    tokens_ref,
    gain_ref,
    wq_ref,
    wk_ref,
    wv_ref,
    wo_ref,
    cache_ref,
    expo_ref,
    cos_ref,
    sin_ref,
    bias_ref,
    out_ref,
    slots,
    sums,
    wq,
    wk,
    wv,
    wo,
    heads,
    key_new,
    value_new,
    keys,
    values,
    raw,
    wide,
    expo,
    scale,
    local_sem,
    raw_sem,
    expo_sem,
    out_sem,
    gather_send,
    gather_recv,
    reduce_send,
    reduce_recv,
):
    unit = 2 * PIECE
    units = ranks * batches
    own_rows = unit * batches
    depth = slots.shape[2]
    q_cols = heads.shape[1]
    kv_heads = key_new.shape[1] // HD
    group = q_cols // (kv_heads * HD)
    cache_len = cache_ref.shape[1]
    cache_rows = SEQ_BLOCK * cache_len
    groups = expo_ref.shape[1]
    group_cols = depth // groups
    inv_root = 1.0 / HD**0.5

    me = lax.axis_index("tensor")
    place = ring_index(me, ranks)
    right = ring_index(lax.rem(place + 1, ranks), ranks)
    left = ring_index(lax.rem(place + ranks - 1, ranks), ranks)

    def piece_row(k, d):
        hop, batch = k // batches, k % batches
        source = lax.rem(place + ranks - hop, ranks) if d == 0 else lax.rem(place + hop, ranks)
        return ring_index(source, ranks) * own_rows + (2 * batch + d) * PIECE

    weight_copies = [
        pltpu.make_async_copy(src, dst, local_sem.at[i])
        for i, (src, dst) in enumerate(
            ((wq_ref, wq), (wk_ref, wk), (wv_ref, wv), (wo_ref, wo))
        )
    ]

    def token_copy(b, slot, sem):
        return pltpu.make_async_copy(
            tokens_ref.at[pl.ds(b * unit, unit), :], slots.at[slot], sem
        )

    def out_copy(b, slot):
        return pltpu.make_async_copy(
            slots.at[slot], out_ref.at[pl.ds(b * unit, unit), :], out_sem.at[b]
        )

    def raw_copy(k, d, kv):
        first = piece_row(k, d) // NEW
        return pltpu.make_async_copy(
            cache_ref.at[pl.ds(first, SEQ_BLOCK), :, :, pl.ds(kv * HD, HD)],
            raw.at[d * kv_heads + kv],
            raw_sem.at[d, kv],
        )

    def expo_copy(k, d):
        first = pl.multiple_of(piece_row(k, d), PIECE)
        return pltpu.make_async_copy(
            expo_ref.at[pl.ds(first, PIECE), :],
            expo.at[pl.ds(d * PIECE, PIECE), :],
            expo_sem.at[d],
        )

    def half(d):
        return pl.ds(d * PIECE, PIECE)

    def gather_copy(k, d):
        return pltpu.make_async_remote_copy(
            src_ref=slots.at[k + batches, half(d), :],
            dst_ref=slots.at[k + 2 * batches, half(d), :],
            send_sem=gather_send.at[k, d],
            recv_sem=gather_recv.at[k, d],
            device_id={"tensor": right if d == 0 else left},
            device_id_type=MESH,
        )

    def reduce_copy(k, d):
        return pltpu.make_async_remote_copy(
            src_ref=slots.at[k, half(d), :],
            dst_ref=sums.at[k - batches, half(d), :],
            send_sem=reduce_send.at[k - batches, d],
            recv_sem=reduce_recv.at[k - batches, d],
            device_id={"tensor": right if d == 0 else left},
            device_id_type=MESH,
        )

    for b in range(batches):
        token_copy(b, batches + b, out_sem.at[b]).start()
    for copy in weight_copies:
        copy.start()
    for d in range(2):
        for kv in range(kv_heads):
            raw_copy(0, d, kv).start()
        expo_copy(0, d).start()

    barrier = pltpu.get_barrier_semaphore()
    for neighbour in (left, right):
        pl.semaphore_signal(
            barrier, inc=1, device_id={"tensor": neighbour}, device_id_type=MESH
        )

    def norm(slot, d):
        def step(i, carry):
            rows = pl.ds(pl.multiple_of(d * PIECE + i * 16, 16), 16)
            floats = slots[slot, rows, :].astype(jnp.float32)
            normed = floats * lax.rsqrt(jnp.mean(floats * floats, axis=-1, keepdims=True) + epsilon)
            slots[slot, rows, :] = (normed * gain_ref[...].astype(jnp.float32)).astype(jnp.bfloat16)
            return carry

        lax.fori_loop(0, PIECE // 16, step, 0)

    token_copy(0, batches, out_sem.at[0]).wait()
    norm(batches, 0)
    norm(batches, 1)
    pl.semaphore_wait(barrier, 2)
    for d in range(2):
        gather_copy(0, d).start()
    for b in range(1, batches):
        token_copy(b, batches + b, out_sem.at[b]).wait()
        for d in range(2):
            norm(batches + b, d)
            gather_copy(b, d).start()

    def turn(block):
        cosine = cos_ref[...]
        sine_part = sin_ref[...]
        parts = []
        for d in range(2):
            turned = []
            for h in range(block.shape[1] // HD):
                head = block[d * PIECE : (d + 1) * PIECE, h * HD : (h + 1) * HD]
                turned.append(head * cosine + pltpu.roll(head, HD // 2, 1) * sine_part)
            parts.append(jnp.concatenate(turned, 1) if len(turned) > 1 else turned[0])
        return jnp.concatenate(parts, 0)

    def project(k):
        slot = k + batches
        width = min(WIDTH, q_cols)

        def tile(j, carry):
            cols = pl.ds(pl.multiple_of(j * width, width), width)
            query = jnp.dot(slots[slot], wq[:, cols], preferred_element_type=jnp.float32)
            heads[:, cols] = turn(query).astype(jnp.bfloat16)
            return carry

        lax.fori_loop(0, q_cols // width, tile, 0)
        key = jnp.dot(slots[slot], wk[...], preferred_element_type=jnp.float32)
        key_new[...] = turn(key).astype(jnp.bfloat16)
        value = jnp.dot(slots[slot], wv[...], preferred_element_type=jnp.float32)
        value_new[...] = value.astype(jnp.bfloat16)

    def attend(k, d):
        rows = half(d)
        bias = bias_ref[...]
        for kv in range(kv_heads):
            raw_copy(k, d, kv).wait()
            span = slice(kv * HD, (kv + 1) * HD)
            wide[...] = raw.at[d * kv_heads + kv].reshape(2 * cache_rows, HD)[...].astype(jnp.float32)
            keys[:cache_rows] = wide[pl.ds(0, cache_rows, 2), :].astype(jnp.bfloat16)
            values[:cache_rows] = wide[pl.ds(1, cache_rows, 2), :].astype(jnp.bfloat16)
            keys[cache_rows:] = key_new[rows, span]
            values[cache_rows:] = value_new[rows, span]

            @pl.when(k + 1 < units)
            def _():
                raw_copy(k + 1, d, kv).start()

            base = kv * group * HD
            query = jnp.concatenate(
                [heads[rows, base + g * HD : base + (g + 1) * HD] for g in range(group)], 0
            )
            scores = lax.dot_general(
                query, keys[...], (((1,), (1,)), ((), ())), preferred_element_type=jnp.float32
            )
            weights = []
            for g in range(group):
                part = scores[g * PIECE : (g + 1) * PIECE] * inv_root + bias
                probs = jnp.exp(part - jnp.max(part, axis=-1, keepdims=True))
                total = 1.0 / jnp.sum(probs, axis=-1, keepdims=True)
                weights.append((probs * total).astype(jnp.bfloat16))
            combined = jnp.dot(
                jnp.concatenate(weights, 0), values[...], preferred_element_type=jnp.float32
            ).astype(jnp.bfloat16)
            for g in range(group):
                heads[rows, base + g * HD : base + (g + 1) * HD] = combined[
                    g * PIECE : (g + 1) * PIECE
                ]

    def project_out(k):
        for d in range(2):
            expo_copy(k, d).wait()
        scale[:, :groups] = jnp.exp2(-expo[...].astype(jnp.float32))

        @pl.when(k + 1 < units)
        def _():
            for d in range(2):
                expo_copy(k + 1, d).start()

        per_tile = WIDTH // group_cols

        def tile(j, carry):
            cols = pl.ds(pl.multiple_of(j * WIDTH, WIDTH), WIDTH)
            partial_value = jnp.dot(heads[...], wo[:, cols], preferred_element_type=jnp.float32)
            shrink = scale[...]
            parts = []
            for i in range(per_tile):
                part = partial_value[:, i * group_cols : (i + 1) * group_cols]
                parts.append(jnp.clip(part * shrink[:, i : i + 1], -127.0, 127.0))
            slots[k, :, cols] = jnp.concatenate(parts, 1).astype(jnp.bfloat16)
            scale[...] = pltpu.roll(shrink, shrink.shape[1] - per_tile, 1)
            return carry

        lax.fori_loop(0, depth // WIDTH, tile, 0)

    def add_sums(k):
        def step(i, carry):
            rows = pl.ds(pl.multiple_of(i * 16, 16), 16)
            slots[k, rows, :] = (
                slots[k, rows, :].astype(jnp.float32)
                + sums[k - 2 * batches, rows, :].astype(jnp.float32)
            ).astype(jnp.bfloat16)
            return carry

        lax.fori_loop(0, unit // 16, step, 0)

    def body(k, carry):
        @pl.when(k >= units - batches)
        def _():
            for d in range(2):
                gather_copy(k - batches, d).wait_recv()

        @pl.when(k == 0)
        def _():
            for copy in weight_copies[:3]:
                copy.wait()

        project(k)
        for d in range(2):
            attend(k, d)

        @pl.when(k == 0)
        def _():
            weight_copies[3].wait()

        @pl.when(k >= batches)
        def _():
            for d in range(2):
                gather_copy(k - batches, d).wait_send()

        project_out(k)

        @pl.when(k + 2 * batches < units)
        def _():
            for d in range(2):
                gather_copy(k, d).wait_recv()
                gather_copy(k + batches, d).start()

        @pl.when(k >= 2 * batches)
        def _():
            for d in range(2):
                reduce_copy(k - batches, d).wait_recv()
            add_sums(k)

        @pl.when(k >= batches)
        def _():
            for d in range(2):
                reduce_copy(k, d).start()

        return carry

    lax.fori_loop(0, units, body, 0)

    for b in range(batches):
        token_copy(b, units + b, out_sem.at[b]).start()
    for b in range(batches):
        for d in range(2):
            expo_copy(b, d).start()
        token_copy(b, units + b, out_sem.at[b]).wait()
        for d in range(2):
            expo_copy(b, d).wait()
        scale[:, :groups] = jnp.exp2(expo[...].astype(jnp.float32))
        for d in range(2):
            reduce_copy(units - batches + b, d).wait_recv()

            def step(i, carry):
                rows = pl.ds(pl.multiple_of(d * PIECE + i * 16, 16), 16)
                for g in range(groups):
                    cols = slice(g * group_cols, (g + 1) * group_cols)
                    total = slots[b, rows, cols].astype(jnp.float32) + sums[
                        units - 2 * batches + b, rows, cols
                    ].astype(jnp.float32)
                    term = total * scale[rows, g : g + 1]
                    slots[units + b, rows, cols] = (
                        slots[units + b, rows, cols].astype(jnp.float32) + term
                    ).astype(jnp.bfloat16)
                return carry

            lax.fori_loop(0, PIECE // 16, step, 0)
        out_copy(b, units + b).start()
    for b in range(batches):
        out_copy(b, units + b).wait()

    def drain(k, carry):
        for d in range(2):
            reduce_copy(k, d).wait_send()
        return carry

    lax.fori_loop(batches, units, drain, 0)


def on_device(
    tokens, norm_gain, query_weight, key_weight, value_weight, out_weight, past_cache, exponents
):
    own_rows, depth = tokens.shape
    ranks = lax.axis_size("tensor")
    unit = 2 * PIECE
    batches = own_rows // unit
    units = ranks * batches
    q_cols = query_weight.shape[1]
    k_cols = key_weight.shape[1]
    kv_heads = k_cols // HD
    cache_len = past_cache.shape[1]
    cache_rows = SEQ_BLOCK * cache_len
    cosine, sine_part = rotary_tables(cache_len)
    bias = mask_table(cache_len)
    any_spec = pl.BlockSpec(memory_space=pl.ANY)
    vmem_spec = pl.BlockSpec(memory_space=pltpu.VMEM)
    bf16 = jnp.bfloat16
    dma = pltpu.SemaphoreType.DMA
    return pl.pallas_call(
        functools.partial(layer_kernel, ranks, batches),
        in_specs=[any_spec, vmem_spec] + [any_spec] * 6 + [vmem_spec] * 3,
        out_specs=any_spec,
        out_shape=jax.ShapeDtypeStruct(tokens.shape, bf16),
        scratch_shapes=[
            pltpu.VMEM((units + batches, unit, depth), bf16),
            pltpu.VMEM((units - batches, unit, depth), bf16),
            pltpu.VMEM((depth, q_cols), bf16),
            pltpu.VMEM((depth, k_cols), bf16),
            pltpu.VMEM((depth, k_cols), bf16),
            pltpu.VMEM((q_cols, depth), bf16),
            pltpu.VMEM((unit, q_cols), bf16),
            pltpu.VMEM((unit, k_cols), bf16),
            pltpu.VMEM((unit, k_cols), bf16),
            pltpu.VMEM((cache_rows + PIECE, HD), bf16),
            pltpu.VMEM((cache_rows + PIECE, HD), bf16),
            pltpu.VMEM((2 * kv_heads, SEQ_BLOCK, cache_len, 2, HD), bf16),
            pltpu.VMEM((2 * cache_rows, HD), jnp.float32),
            pltpu.VMEM((unit, exponents.shape[1]), jnp.int32),
            pltpu.VMEM((unit, 128), jnp.float32),
            dma((4,)),
            dma((2, kv_heads)),
            dma((2,)),
            dma((batches,)),
            dma((units - batches, 2)),
            dma((units - batches, 2)),
            dma((units - batches, 2)),
            dma((units - batches, 2)),
        ],
        compiler_params=pltpu.CompilerParams(
            collective_id=0, has_side_effects=True, vmem_limit_bytes=67043328
        ),
    )(
        tokens,
        norm_gain.reshape(1, depth),
        query_weight,
        key_weight,
        value_weight,
        out_weight,
        past_cache,
        exponents,
        cosine,
        sine_part,
        bias,
    )


def solution(mesh):
    return jax.shard_map(
        on_device,
        mesh=mesh,
        in_specs=(
            P(("dp", "tensor"), None),
            P(),
            P(None, "tensor"),
            P(None, "tensor"),
            P(None, "tensor"),
            P("tensor", None),
            P("dp", None, None, "tensor"),
            P("dp", None),
        ),
        out_specs=P(("dp", "tensor"), None),
        check_vma=False,
    )
```

time: 280 us -> 192 us (0.69)
  waiting for transfers between devices: 115 us -> 0 us
  Pallas kernels: 131 us -> 185 us
  between operations: 13.2 us -> 0.01 us
  local copies, waits for them, and re-layouts: 16.2 us -> 6.82 us
  other arithmetic: 4.02 us -> 0 us
    reduce_scatter x2 -> x0, waiting for transfers between devices: 68.2 us -> none  [on_device(): lax.psum_scatter(rounded, 'tensor', scatter_dimension=0, tiled=True)]
    pallas_call x9 -> x1, Pallas kernels: 131 us -> 185 us  [on_device(): pl.pallas_call(functools.partial(layer_kernel, ranks, batches), in_specs=...]
    all_gather x2 -> x0, waiting for transfers between devices: 46.5 us -> none  [on_device(): gathered.append(lax.all_gather(normed, 'tensor', axis=0, tiled=True))]
    another operation x4 -> x0, local copies, waits for them, and re-layouts: 4.84 us -> none  [project_out(): shrink.reshape(rows, groups // per_block, per_block).transpose(1, 0, 2)]
    unnamed x4 -> x2, local copies, waits for them, and re-layouts: 8.77 us -> 5.52 us
  transfers between devices with their start and end apart: 4 -> 0, of which waited for: 4 -> 0; matrix products, arithmetic and copies ran while one was open for 7% -> 0% of each run, Pallas kernels for 44% -> 0%
where the time goes in v1:
time: 192 us
  Pallas kernels  185 us (96%)
  local copies, waits for them, and re-layouts  6.82 us (4%)
    pallas_call x1, Pallas kernels, on_device(): pl.pallas_call(functools.partial(layer_kernel, ranks, batches), in_specs=...  185 us
    unnamed x2, local copies, waits for them, and re-layouts  5.52 us

profile of v1, /device:TPU:0, one launch (start us, length us, event | category | flops | bytes accessed | tf_op | source)
XLA Modules:
  0.0 191.6 jit_solution(8004341758254784086)
XLA Ops:
  0.0 1.3 reshape.3.gain_ref
  1.3 2.0 %copy.12.expo_ref = s32[1280,32]{1,0:T(8,128)} copy(s32[1280,32]{0,1:T(8,128)} %param.18) | data formatting | bytes 327680 | tf_op args[7]
  3.3 184.7 %shard_map.109 = bf16[320,4096]{1,0:T(8,128)(2,1)} custom-call(bf16[320,4096]{1,0:T(8,128)(2,1)} %tokens_ref.1, bf16[1,4096]{1,0:T(2,128)(2,1)} %reshape.3.gain_ref, bf16[4096,2048]{1,0:T(8,128)(2,1)} %wq_ref.1, bf16[4096,256]{1,0:T(8,128)(2,1)} %wk_ref.1, bf16[4096,256]{1,0:T(8,128)(2,1)} %wv_ref.1, bf16[2048,4096]{1,0:T(8,128)(2,1)} %wo_ref.1, ...), custom_call_target="tpu_custom_call" | custom-call | tf_op jit(solution)/shard_map/pallas_call | solution.py:410
  188.0 3.5 %copy.14 = bf16[320,4096]{1,0:T(8,128)(2,1)} copy(bf16[320,4096]{1,0:T(8,128)(2,1)} %shard_map.109) | data formatting | bytes 5242880

commit v2 on v1

--- a/solution.py
+++ b/solution.py
@@ -13,6 +13,8 @@
 SEQ_BLOCK = 8
 PIECE = SEQ_BLOCK * NEW
 WIDTH = 512
+SPLIT = 2
+LAST = ((0, 48), (48, 32))
 
 epsilon = 1e-05
 theta_base = 500000.0
@@ -74,16 +76,19 @@
     values,
     raw,
     wide,
-    expo,
+    gain,
+    powers,
     scale,
     local_sem,
     raw_sem,
-    expo_sem,
+    token_sem,
     out_sem,
     gather_send,
     gather_recv,
     reduce_send,
     reduce_recv,
+    last_send,
+    last_recv,
 ):
     unit = 2 * PIECE
     units = ranks * batches
@@ -94,7 +99,7 @@
     group = q_cols // (kv_heads * HD)
     cache_len = cache_ref.shape[1]
     cache_rows = SEQ_BLOCK * cache_len
-    groups = expo_ref.shape[1]
+    groups = expo_ref.shape[0]
     group_cols = depth // groups
     inv_root = 1.0 / HD**0.5
 
@@ -103,6 +108,9 @@
     right = ring_index(lax.rem(place + 1, ranks), ranks)
     left = ring_index(lax.rem(place + ranks - 1, ranks), ranks)
 
+    def half(d):
+        return pl.ds(d * PIECE, PIECE)
+
     def piece_row(k, d):
         hop, batch = k // batches, k % batches
         source = lax.rem(place + ranks - hop, ranks) if d == 0 else lax.rem(place + hop, ranks)
@@ -115,14 +123,36 @@
         )
     ]
 
-    def token_copy(b, slot, sem):
+    def first_copy(b, d):
         return pltpu.make_async_copy(
-            tokens_ref.at[pl.ds(b * unit, unit), :], slots.at[slot], sem
-        )
-
-    def out_copy(b, slot):
+            tokens_ref.at[pl.ds(b * unit + d * PIECE, PIECE), :],
+            slots.at[batches + b, half(d), :],
+            token_sem.at[b, d],
+        )
+
+    def token_copy(b):
         return pltpu.make_async_copy(
-            slots.at[slot], out_ref.at[pl.ds(b * unit, unit), :], out_sem.at[b]
+            tokens_ref.at[pl.ds(b * unit, unit), :], slots.at[units + b], token_sem.at[b, 0]
+        )
+
+    def out_copy(b, d, part):
+        first, size = LAST[part]
+        return pltpu.make_async_copy(
+            slots.at[units + b, pl.ds(d * PIECE + first, size), :],
+            out_ref.at[pl.ds(b * unit + d * PIECE + first, size), :],
+            out_sem.at[b, d, part],
+        )
+
+    def last_copy(k, d, part):
+        first, size = LAST[part]
+        rows = pl.ds(d * PIECE + first, size)
+        return pltpu.make_async_remote_copy(
+            src_ref=slots.at[k, rows, :],
+            dst_ref=sums.at[k - batches, rows, :],
+            send_sem=last_send.at[k - units + batches, d, part],
+            recv_sem=last_recv.at[k - units + batches, d, part],
+            device_id={"tensor": right if d == 0 else left},
+            device_id_type=MESH,
         )
 
     def raw_copy(k, d, kv):
@@ -133,16 +163,8 @@
             raw_sem.at[d, kv],
         )
 
-    def expo_copy(k, d):
-        first = pl.multiple_of(piece_row(k, d), PIECE)
-        return pltpu.make_async_copy(
-            expo_ref.at[pl.ds(first, PIECE), :],
-            expo.at[pl.ds(d * PIECE, PIECE), :],
-            expo_sem.at[d],
-        )
-
-    def half(d):
-        return pl.ds(d * PIECE, PIECE)
+    def power_rows(k, d):
+        return powers[pl.ds(pl.multiple_of(piece_row(k, d), PIECE), PIECE), :].astype(jnp.float32)
 
     def gather_copy(k, d):
         return pltpu.make_async_remote_copy(
@@ -164,14 +186,8 @@
             device_id_type=MESH,
         )
 
-    for b in range(batches):
-        token_copy(b, batches + b, out_sem.at[b]).start()
-    for copy in weight_copies:
-        copy.start()
     for d in range(2):
-        for kv in range(kv_heads):
-            raw_copy(0, d, kv).start()
-        expo_copy(0, d).start()
+        first_copy(0, d).start()
 
     barrier = pltpu.get_barrier_semaphore()
     for neighbour in (left, right):
@@ -184,22 +200,38 @@
             rows = pl.ds(pl.multiple_of(d * PIECE + i * 16, 16), 16)
             floats = slots[slot, rows, :].astype(jnp.float32)
             normed = floats * lax.rsqrt(jnp.mean(floats * floats, axis=-1, keepdims=True) + epsilon)
-            slots[slot, rows, :] = (normed * gain_ref[...].astype(jnp.float32)).astype(jnp.bfloat16)
+            slots[slot, rows, :] = (normed * gain[...]).astype(jnp.bfloat16)
             return carry
 
         lax.fori_loop(0, PIECE // 16, step, 0)
 
-    token_copy(0, batches, out_sem.at[0]).wait()
-    norm(batches, 0)
-    norm(batches, 1)
-    pl.semaphore_wait(barrier, 2)
+    gain[...] = gain_ref[...].astype(jnp.float32).reshape(1, depth)
     for d in range(2):
+        first_copy(0, d).wait()
+        if d == 0:
+            for b in range(1, batches):
+                for e in range(2):
+                    first_copy(b, e).start()
+            for copy in weight_copies:
+                copy.start()
+        norm(batches, d)
+        if d == 0:
+            pl.semaphore_wait(barrier, 2)
         gather_copy(0, d).start()
+    for d in range(2):
+        for kv in range(kv_heads):
+            raw_copy(0, d, kv).start()
     for b in range(1, batches):
-        token_copy(b, batches + b, out_sem.at[b]).wait()
         for d in range(2):
+            first_copy(b, d).wait()
             norm(batches + b, d)
             gather_copy(b, d).start()
+    token_total = powers.shape[0]
+    for first in range(0, token_total, 128):
+        size = min(128, token_total - first)
+        block = expo_ref[:, first : first + size].astype(jnp.float32)
+        block = jnp.concatenate([block, jnp.zeros((128 - groups, size), jnp.float32)], 0)
+        powers[first : first + size, :] = block.T.astype(jnp.bfloat16)
 
     def turn(block):
         cosine = cos_ref[...]
@@ -235,9 +267,13 @@
         for kv in range(kv_heads):
             raw_copy(k, d, kv).wait()
             span = slice(kv * HD, (kv + 1) * HD)
-            wide[...] = raw.at[d * kv_heads + kv].reshape(2 * cache_rows, HD)[...].astype(jnp.float32)
-            keys[:cache_rows] = wide[pl.ds(0, cache_rows, 2), :].astype(jnp.bfloat16)
-            values[:cache_rows] = wide[pl.ds(1, cache_rows, 2), :].astype(jnp.bfloat16)
+            pairs = raw.at[d * kv_heads + kv].reshape(2 * cache_rows, HD)
+            some = cache_rows // 2
+            for part in range(2):
+                wide[...] = pairs[part * cache_rows : (part + 1) * cache_rows].astype(jnp.float32)
+                span_rows = slice(part * some, (part + 1) * some)
+                keys[span_rows] = wide[pl.ds(0, some, 2), :].astype(jnp.bfloat16)
+                values[span_rows] = wide[pl.ds(1, some, 2), :].astype(jnp.bfloat16)
             keys[cache_rows:] = key_new[rows, span]
             values[cache_rows:] = value_new[rows, span]
 
@@ -246,35 +282,32 @@
                 raw_copy(k + 1, d, kv).start()
 
             base = kv * group * HD
-            query = jnp.concatenate(
-                [heads[rows, base + g * HD : base + (g + 1) * HD] for g in range(group)], 0
-            )
-            scores = lax.dot_general(
-                query, keys[...], (((1,), (1,)), ((), ())), preferred_element_type=jnp.float32
-            )
-            weights = []
-            for g in range(group):
-                part = scores[g * PIECE : (g + 1) * PIECE] * inv_root + bias
-                probs = jnp.exp(part - jnp.max(part, axis=-1, keepdims=True))
-                total = 1.0 / jnp.sum(probs, axis=-1, keepdims=True)
-                weights.append((probs * total).astype(jnp.bfloat16))
-            combined = jnp.dot(
-                jnp.concatenate(weights, 0), values[...], preferred_element_type=jnp.float32
-            ).astype(jnp.bfloat16)
-            for g in range(group):
-                heads[rows, base + g * HD : base + (g + 1) * HD] = combined[
-                    g * PIECE : (g + 1) * PIECE
-                ]
+            count = max(group // SPLIT, 1)
+            for first in range(0, group, count):
+                start = base + first * HD
+                query = jnp.concatenate(
+                    [heads[rows, start + g * HD : start + (g + 1) * HD] for g in range(count)], 0
+                )
+                scores = lax.dot_general(
+                    query, keys[...], (((1,), (1,)), ((), ())), preferred_element_type=jnp.float32
+                )
+                weights = []
+                for g in range(count):
+                    part = scores[g * PIECE : (g + 1) * PIECE] * inv_root + bias
+                    probs = jnp.exp(part - jnp.max(part, axis=-1, keepdims=True))
+                    total = 1.0 / jnp.sum(probs, axis=-1, keepdims=True)
+                    weights.append((probs * total).astype(jnp.bfloat16))
+                combined = jnp.dot(
+                    jnp.concatenate(weights, 0), values[...], preferred_element_type=jnp.float32
+                ).astype(jnp.bfloat16)
+                for g in range(count):
+                    heads[rows, start + g * HD : start + (g + 1) * HD] = combined[
+                        g * PIECE : (g + 1) * PIECE
+                    ]
 
     def project_out(k):
         for d in range(2):
-            expo_copy(k, d).wait()
-        scale[:, :groups] = jnp.exp2(-expo[...].astype(jnp.float32))
-
-        @pl.when(k + 1 < units)
-        def _():
-            for d in range(2):
-                expo_copy(k + 1, d).start()
+            scale[half(d), :] = jnp.exp2(-power_rows(k, d))
 
         per_tile = WIDTH // group_cols
 
@@ -318,74 +351,81 @@
         for d in range(2):
             attend(k, d)
 
-        @pl.when(k == 0)
-        def _():
-            weight_copies[3].wait()
-
-        @pl.when(k >= batches)
-        def _():
-            for d in range(2):
-                gather_copy(k - batches, d).wait_send()
-
-        project_out(k)
-
         @pl.when(k + 2 * batches < units)
         def _():
             for d in range(2):
                 gather_copy(k, d).wait_recv()
                 gather_copy(k + batches, d).start()
 
+        @pl.when(k == 0)
+        def _():
+            weight_copies[3].wait()
+
+        @pl.when(k >= batches)
+        def _():
+            for d in range(2):
+                gather_copy(k - batches, d).wait_send()
+
+        project_out(k)
+
         @pl.when(k >= 2 * batches)
         def _():
             for d in range(2):
                 reduce_copy(k - batches, d).wait_recv()
             add_sums(k)
 
-        @pl.when(k >= batches)
+        @pl.when((k >= batches) & (k < units - batches))
         def _():
             for d in range(2):
                 reduce_copy(k, d).start()
 
+        @pl.when(k >= units - batches)
+        def _():
+            for part in range(len(LAST)):
+                for d in range(2):
+                    last_copy(k, d, part).start()
+
         return carry
 
     lax.fori_loop(0, units, body, 0)
 
     for b in range(batches):
-        token_copy(b, units + b, out_sem.at[b]).start()
+        token_copy(b).start()
     for b in range(batches):
+        token_copy(b).wait()
         for d in range(2):
-            expo_copy(b, d).start()
-        token_copy(b, units + b, out_sem.at[b]).wait()
-        for d in range(2):
-            expo_copy(b, d).wait()
-        scale[:, :groups] = jnp.exp2(expo[...].astype(jnp.float32))
-        for d in range(2):
-            reduce_copy(units - batches + b, d).wait_recv()
-
-            def step(i, carry):
-                rows = pl.ds(pl.multiple_of(d * PIECE + i * 16, 16), 16)
-                for g in range(groups):
-                    cols = slice(g * group_cols, (g + 1) * group_cols)
-                    total = slots[b, rows, cols].astype(jnp.float32) + sums[
-                        units - 2 * batches + b, rows, cols
-                    ].astype(jnp.float32)
-                    term = total * scale[rows, g : g + 1]
-                    slots[units + b, rows, cols] = (
-                        slots[units + b, rows, cols].astype(jnp.float32) + term
-                    ).astype(jnp.bfloat16)
-                return carry
-
-            lax.fori_loop(0, PIECE // 16, step, 0)
-        out_copy(b, units + b).start()
-    for b in range(batches):
-        out_copy(b, units + b).wait()
+            scale[half(d), :] = jnp.exp2(power_rows(b, d))
+        for part, (first, size) in enumerate(LAST):
+            for d in range(2):
+                last_copy(units - batches + b, d, part).wait_recv()
+
+                def step(i, carry):
+                    rows = pl.ds(pl.multiple_of(d * PIECE + first + i * 16, 16), 16)
+                    for g in range(groups):
+                        cols = slice(g * group_cols, (g + 1) * group_cols)
+                        total = slots[b, rows, cols].astype(jnp.float32) + sums[
+                            units - 2 * batches + b, rows, cols
+                        ].astype(jnp.float32)
+                        term = total * scale[rows, g : g + 1]
+                        slots[units + b, rows, cols] = (
+                            slots[units + b, rows, cols].astype(jnp.float32) + term
+                        ).astype(jnp.bfloat16)
+                    return carry
+
+                lax.fori_loop(0, size // 16, step, 0)
+                out_copy(b, d, part).start()
 
     def drain(k, carry):
         for d in range(2):
             reduce_copy(k, d).wait_send()
         return carry
 
-    lax.fori_loop(batches, units, drain, 0)
+    lax.fori_loop(batches, units - batches, drain, 0)
+    for b in range(batches):
+        for part in range(len(LAST)):
+            for d in range(2):
+                last_copy(units - batches + b, d, part).wait_send()
+                out_copy(b, d, part).wait()
 
 
 def on_device(
@@ -409,7 +449,7 @@
     dma = pltpu.SemaphoreType.DMA
     return pl.pallas_call(
         functools.partial(layer_kernel, ranks, batches),
-        in_specs=[any_spec, vmem_spec] + [any_spec] * 6 + [vmem_spec] * 3,
+        in_specs=[any_spec, vmem_spec] + [any_spec] * 5 + [vmem_spec] * 4,
         out_specs=any_spec,
         out_shape=jax.ShapeDtypeStruct(tokens.shape, bf16),
         scratch_shapes=[
@@ -425,30 +465,33 @@
             pltpu.VMEM((cache_rows + PIECE, HD), bf16),
             pltpu.VMEM((cache_rows + PIECE, HD), bf16),
             pltpu.VMEM((2 * kv_heads, SEQ_BLOCK, cache_len, 2, HD), bf16),
-            pltpu.VMEM((2 * cache_rows, HD), jnp.float32),
-            pltpu.VMEM((unit, exponents.shape[1]), jnp.int32),
+            pltpu.VMEM((cache_rows, HD), jnp.float32),
+            pltpu.VMEM((1, depth), jnp.float32),
+            pltpu.VMEM((exponents.shape[0], 128), bf16),
             pltpu.VMEM((unit, 128), jnp.float32),
             dma((4,)),
             dma((2, kv_heads)),
-            dma((2,)),
-            dma((batches,)),
+            dma((batches, 2)),
+            dma((batches, 2, len(LAST))),
             dma((units - batches, 2)),
             dma((units - batches, 2)),
             dma((units - batches, 2)),
             dma((units - batches, 2)),
+            dma((batches, 2, len(LAST))),
+            dma((batches, 2, len(LAST))),
         ],
         compiler_params=pltpu.CompilerParams(
             collective_id=0, has_side_effects=True, vmem_limit_bytes=67043328
         ),
     )(
         tokens,
-        norm_gain.reshape(1, depth),
+        norm_gain,
         query_weight,
         key_weight,
         value_weight,
         out_weight,
         past_cache,
-        exponents,
+        exponents.T,
         cosine,
         sine_part,
         bias,

time: 192 us -> 181 us (0.943)
  Pallas kernels: 185 us -> 178 us
  local copies, waits for them, and re-layouts: 6.82 us -> 3.53 us
    pallas_call x1, Pallas kernels: 185 us -> 178 us  [on_device(): pl.pallas_call(functools.partial(layer_kernel, ranks, batches), in_specs=...]
    unnamed x2 -> x1, local copies, waits for them, and re-layouts: 5.52 us -> 3.53 us
where the time goes in v2:
time: 181 us
  Pallas kernels  178 us (98%)
  local copies, waits for them, and re-layouts  3.53 us (2%)
    pallas_call x1, Pallas kernels, on_device(): pl.pallas_call(functools.partial(layer_kernel, ranks, batches), in_specs=...  178 us

profile of v2, /device:TPU:0, one launch (start us, length us, event | category | flops | bytes accessed | tf_op | source)
XLA Modules:
  0.0 181.1 jit_solution(203406741391891479)
XLA Ops:
  0.0 177.6 %shard_map.109 = bf16[320,4096]{1,0:T(8,128)(2,1)} custom-call(bf16[320,4096]{1,0:T(8,128)(2,1)} %tokens_ref.1, bf16[4096]{0:T(1024)(128)(2,1)} %gain_ref.1, bf16[4096,2048]{1,0:T(8,128)(2,1)} %wq_ref.1, bf16[4096,256]{1,0:T(8,128)(2,1)} %wk_ref.1, bf16[4096,256]{1,0:T(8,128)(2,1)} %wv_ref.1, bf16[2048,4096]{1,0:T(8,128)(2,1)} %wo_ref.1, ...), custom_call_target="tpu_custom_call" | custom-call | tf_op jit(solution)/shard_map/pallas_call | solution.py:450
  177.6 3.5 %copy.13 = bf16[320,4096]{1,0:T(8,128)(2,1)} copy(bf16[320,4096]{1,0:T(8,128)(2,1)} %shard_map.109) | data formatting | bytes 5242880

commit v3 on v2

--- a/solution.py
+++ b/solution.py
@@ -14,7 +14,9 @@
 PIECE = SEQ_BLOCK * NEW
 WIDTH = 512
 SPLIT = 2
-LAST = ((0, 48), (48, 32))
+FIRST = ((0, 16), (16, 32), (48, 32))
+LAST = ((0, 48), (48, 16), (64, 16))
+COPY_ROWS = 32
 
 epsilon = 1e-05
 theta_base = 500000.0
@@ -52,16 +54,16 @@
     ranks,
     batches,
     tokens_ref,
-    gain_ref,
+    gain_in,
     wq_ref,
     wk_ref,
     wv_ref,
     wo_ref,
     cache_ref,
-    expo_ref,
-    cos_ref,
-    sin_ref,
-    bias_ref,
+    expo_in,
+    cos_in,
+    sin_in,
+    bias_in,
     out_ref,
     slots,
     sums,
@@ -76,10 +78,16 @@
     values,
     raw,
     wide,
+    gain_ref,
+    expo_ref,
+    cos_ref,
+    sin_ref,
+    bias_ref,
     gain,
     powers,
     scale,
     local_sem,
+    small_sem,
     raw_sem,
     token_sem,
     out_sem,
@@ -99,7 +107,7 @@
     group = q_cols // (kv_heads * HD)
     cache_len = cache_ref.shape[1]
     cache_rows = SEQ_BLOCK * cache_len
-    groups = expo_ref.shape[0]
+    groups = expo_in.shape[0]
     group_cols = depth // groups
     inv_root = 1.0 / HD**0.5
 
@@ -123,16 +131,30 @@
         )
     ]
 
-    def first_copy(b, d):
+    small_copies = [
+        pltpu.make_async_copy(src, dst, small_sem.at[i])
+        for i, (src, dst) in enumerate(
+            (
+                (gain_in, gain_ref),
+                (expo_in, expo_ref),
+                (cos_in, cos_ref),
+                (sin_in, sin_ref),
+                (bias_in, bias_ref),
+            )
+        )
+    ]
+
+    def first_copy(b, d, part, rows):
+        first, size = rows
         return pltpu.make_async_copy(
-            tokens_ref.at[pl.ds(b * unit + d * PIECE, PIECE), :],
-            slots.at[batches + b, half(d), :],
-            token_sem.at[b, d],
+            tokens_ref.at[pl.ds(b * unit + d * PIECE + first, size), :],
+            slots.at[batches + b, pl.ds(d * PIECE + first, size), :],
+            token_sem.at[b, d, part],
         )
 
     def token_copy(b):
         return pltpu.make_async_copy(
-            tokens_ref.at[pl.ds(b * unit, unit), :], slots.at[units + b], token_sem.at[b, 0]
+            tokens_ref.at[pl.ds(b * unit, unit), :], slots.at[units + b], token_sem.at[b, 0, 0]
         )
 
     def out_copy(b, d, part):
@@ -166,10 +188,11 @@
     def power_rows(k, d):
         return powers[pl.ds(pl.multiple_of(piece_row(k, d), PIECE), PIECE), :].astype(jnp.float32)
 
-    def gather_copy(k, d):
+    def gather_copy(k, d, rows=(0, PIECE)):
+        span = pl.ds(d * PIECE + rows[0], rows[1])
         return pltpu.make_async_remote_copy(
-            src_ref=slots.at[k + batches, half(d), :],
-            dst_ref=slots.at[k + 2 * batches, half(d), :],
+            src_ref=slots.at[k + batches, span, :],
+            dst_ref=slots.at[k + 2 * batches, span, :],
             send_sem=gather_send.at[k, d],
             recv_sem=gather_recv.at[k, d],
             device_id={"tensor": right if d == 0 else left},
@@ -186,46 +209,53 @@
             device_id_type=MESH,
         )
 
-    for d in range(2):
-        first_copy(0, d).start()
-
     barrier = pltpu.get_barrier_semaphore()
     for neighbour in (left, right):
         pl.semaphore_signal(
             barrier, inc=1, device_id={"tensor": neighbour}, device_id_type=MESH
         )
 
-    def norm(slot, d):
+    small_copies[0].start()
+    for part, rows in enumerate(FIRST):
+        for d in range(2):
+            first_copy(0, d, part, rows).start()
+
+    def norm(slot, d, first, size):
         def step(i, carry):
-            rows = pl.ds(pl.multiple_of(d * PIECE + i * 16, 16), 16)
+            rows = pl.ds(pl.multiple_of(d * PIECE + first + i * 16, 16), 16)
             floats = slots[slot, rows, :].astype(jnp.float32)
             normed = floats * lax.rsqrt(jnp.mean(floats * floats, axis=-1, keepdims=True) + epsilon)
             slots[slot, rows, :] = (normed * gain[...]).astype(jnp.bfloat16)
             return carry
 
-        lax.fori_loop(0, PIECE // 16, step, 0)
-
+        lax.fori_loop(0, size // 16, step, 0)
+
+    small_copies[0].wait()
     gain[...] = gain_ref[...].astype(jnp.float32).reshape(1, depth)
-    for d in range(2):
-        first_copy(0, d).wait()
-        if d == 0:
+    whole = (0, PIECE)
+    for part, rows in enumerate(FIRST):
+        for d in range(2):
+            first_copy(0, d, part, rows).wait()
+            norm(batches, d, *rows)
+            if part == 0 and d == 0:
+                pl.semaphore_wait(barrier, 2)
+            gather_copy(0, d, rows).start()
+        if part == 0:
             for b in range(1, batches):
-                for e in range(2):
-                    first_copy(b, e).start()
-            for copy in weight_copies:
+                for d in range(2):
+                    first_copy(b, d, 0, whole).start()
+            for copy in weight_copies + small_copies[1:]:
                 copy.start()
-        norm(batches, d)
-        if d == 0:
-            pl.semaphore_wait(barrier, 2)
-        gather_copy(0, d).start()
-    for d in range(2):
-        for kv in range(kv_heads):
-            raw_copy(0, d, kv).start()
+            for d in range(2):
+                for kv in range(kv_heads):
+                    raw_copy(0, d, kv).start()
     for b in range(1, batches):
         for d in range(2):
-            first_copy(b, d).wait()
-            norm(batches + b, d)
+            first_copy(b, d, 0, whole).wait()
+            norm(batches + b, d, *whole)
             gather_copy(b, d).start()
+    for copy in small_copies[1:]:
+        copy.wait()
     token_total = powers.shape[0]
     for first in range(0, token_total, 128):
         size = min(128, token_total - first)
@@ -428,6 +458,39 @@
                 out_copy(b, d, part).wait()
 
 
+def copy_kernel(src_ref, out_ref, held, in_sem, out_sem):
+    count = src_ref.shape[0] // COPY_ROWS
+
+    def move(src, dst, sem, i):
+        rows = pl.ds(i * COPY_ROWS, COPY_ROWS)
+        return pltpu.make_async_copy(src.at[rows, :], dst.at[rows, :], sem.at[i])
+
+    for i in range(count):
+        move(src_ref, held, in_sem, i).start()
+    for i in range(count):
+        move(src_ref, held, in_sem, i).wait()
+        move(held, out_ref, out_sem, i).start()
+    for i in range(count):
+        move(held, out_ref, out_sem, i).wait()
+
+
+def copy_out(mixed):
+    count = mixed.shape[0] // COPY_ROWS
+    any_spec = pl.BlockSpec(memory_space=pl.ANY)
+    return pl.pallas_call(
+        copy_kernel,
+        in_specs=[any_spec],
+        out_specs=any_spec,
+        out_shape=jax.ShapeDtypeStruct(mixed.shape, mixed.dtype),
+        scratch_shapes=[
+            pltpu.VMEM(mixed.shape, mixed.dtype),
+            pltpu.SemaphoreType.DMA((count,)),
+            pltpu.SemaphoreType.DMA((count,)),
+        ],
+        compiler_params=pltpu.CompilerParams(vmem_limit_bytes=56 * 1024 * 1024),
+    )(mixed)
+
+
 def on_device(
     tokens, norm_gain, query_weight, key_weight, value_weight, out_weight, past_cache, exponents
 ):
@@ -444,12 +507,11 @@
     cosine, sine_part = rotary_tables(cache_len)
     bias = mask_table(cache_len)
     any_spec = pl.BlockSpec(memory_space=pl.ANY)
-    vmem_spec = pl.BlockSpec(memory_space=pltpu.VMEM)
     bf16 = jnp.bfloat16
     dma = pltpu.SemaphoreType.DMA
-    return pl.pallas_call(
+    mixed = pl.pallas_call(
         functools.partial(layer_kernel, ranks, batches),
-        in_specs=[any_spec, vmem_spec] + [any_spec] * 5 + [vmem_spec] * 4,
+        in_specs=[any_spec] * 11,
         out_specs=any_spec,
         out_shape=jax.ShapeDtypeStruct(tokens.shape, bf16),
         scratch_shapes=[
@@ -466,12 +528,18 @@
             pltpu.VMEM((cache_rows + PIECE, HD), bf16),
             pltpu.VMEM((2 * kv_heads, SEQ_BLOCK, cache_len, 2, HD), bf16),
             pltpu.VMEM((cache_rows, HD), jnp.float32),
+            pltpu.VMEM(norm_gain.shape, bf16),
+            pltpu.VMEM(exponents.shape[::-1], jnp.int32),
+            pltpu.VMEM(cosine.shape, jnp.float32),
+            pltpu.VMEM(sine_part.shape, jnp.float32),
+            pltpu.VMEM(bias.shape, jnp.float32),
             pltpu.VMEM((1, depth), jnp.float32),
             pltpu.VMEM((exponents.shape[0], 128), bf16),
             pltpu.VMEM((unit, 128), jnp.float32),
             dma((4,)),
+            dma((5,)),
             dma((2, kv_heads)),
-            dma((batches, 2)),
+            dma((batches, 2, len(FIRST))),
             dma((batches, 2, len(LAST))),
             dma((units - batches, 2)),
             dma((units - batches, 2)),
@@ -496,6 +564,7 @@
         sine_part,
         bias,
     )
+    return copy_out(mixed)
 
 
 def solution(mesh):

time: 181 us -> 178 us (0.983)
  local copies, waits for them, and re-layouts: 3.53 us -> 0 us
    unnamed x1 -> x0, local copies, waits for them, and re-layouts: 3.53 us -> none
    pallas_call x0 -> x1, Pallas kernels: none -> 2.6 us  [copy_out(): pl.pallas_call(copy_kernel, in_specs=[any_spec], out_specs=any_spec, out_...]
    pallas_call x1, Pallas kernels: 178 us -> 175 us  [on_device(): pl.pallas_call(functools.partial(layer_kernel, ranks, batches), in_specs=...]
where the time goes in v3:
time: 178 us
  Pallas kernels  178 us (100%)
    pallas_call x1, Pallas kernels, on_device(): pl.pallas_call(functools.partial(layer_kernel, ranks, batches), in_specs=...  175 us

profile of v3, /device:TPU:0, one launch (start us, length us, event | category | flops | bytes accessed | tf_op | source)
XLA Modules:
  0.0 178.0 jit_solution(1524817808305457034)
XLA Ops:
  0.0 175.4 %shard_map.109.src_ref = bf16[320,4096]{1,0:T(8,128)(2,1)} custom-call(bf16[320,4096]{1,0:T(8,128)(2,1)} %tokens_ref.1, bf16[4096]{0:T(1024)(128)(2,1)} %gain_in.1, bf16[4096,2048]{1,0:T(8,128)(2,1)} %wq_ref.1, bf16[4096,256]{1,0:T(8,128)(2,1)} %wk_ref.1, bf16[4096,256]{1,0:T(8,128)(2,1)} %wv_ref.1, bf16[2048,4096]{1,0:T(8,128)(2,1)} %wo_ref.1, ...), custom_call_target="tpu_custom_call" | custom-call | tf_op jit(solution)/shard_map/pallas_call | solution.py:512
  175.4 2.6 %shard_map.110 = bf16[320,4096]{1,0:T(8,128)(2,1)} custom-call(bf16[320,4096]{1,0:T(8,128)(2,1)} %shard_map.109.src_ref), custom_call_target="tpu_custom_call" | custom-call | tf_op jit(solution)/shard_map/pallas_call | solution.py:480

commit v4 on v3

--- a/solution.py
+++ b/solution.py
@@ -65,6 +65,9 @@
     sin_in,
     bias_in,
     out_ref,
+    tail_own,
+    tail_sum,
+    tail_scale,
     slots,
     sums,
     wq,
@@ -91,6 +94,7 @@
     raw_sem,
     token_sem,
     out_sem,
+    tail_sem,
     gather_send,
     gather_recv,
     reduce_send,
@@ -165,12 +169,12 @@
             out_sem.at[b, d, part],
         )
 
-    def last_copy(k, d, part):
+    def last_copy(k, d, part, tail=False):
         first, size = LAST[part]
         rows = pl.ds(d * PIECE + first, size)
         return pltpu.make_async_remote_copy(
             src_ref=slots.at[k, rows, :],
-            dst_ref=sums.at[k - batches, rows, :],
+            dst_ref=tail_sum.at[d] if tail else sums.at[k - batches, rows, :],
             send_sem=last_send.at[k - units + batches, d, part],
             recv_sem=last_recv.at[k - units + batches, d, part],
             device_id={"tensor": right if d == 0 else left},
@@ -411,13 +415,33 @@
 
         @pl.when(k >= units - batches)
         def _():
-            for part in range(len(LAST)):
+            for part in range(len(LAST) - 1):
                 for d in range(2):
                     last_copy(k, d, part).start()
 
+        @pl.when((k >= units - batches) & (k < units - 1))
+        def _():
+            for d in range(2):
+                last_copy(k, d, len(LAST) - 1).start()
+
+        @pl.when(k == units - 1)
+        def _():
+            for d in range(2):
+                last_copy(k, d, len(LAST) - 1, True).start()
+
         return carry
 
     lax.fori_loop(0, units, body, 0)
+
+    def tail_copies(d):
+        first, size = LAST[-1]
+        rows = pl.ds(d * PIECE + first, size)
+        return (
+            pltpu.make_async_copy(
+                slots.at[batches - 1, rows, :], tail_own.at[d], tail_sem.at[d, 0]
+            ),
+            pltpu.make_async_copy(scale.at[rows, :], tail_scale.at[d], tail_sem.at[d, 1]),
+        )
 
     for b in range(batches):
         token_copy(b).start()
@@ -425,8 +449,14 @@
         token_copy(b).wait()
         for d in range(2):
             scale[half(d), :] = jnp.exp2(power_rows(b, d))
+        if b == batches - 1:
+            for d in range(2):
+                for copy in tail_copies(d):
+                    copy.start()
         for part, (first, size) in enumerate(LAST):
             for d in range(2):
+                if b == batches - 1 and part == len(LAST) - 1:
+                    continue
                 last_copy(units - batches + b, d, part).wait_recv()
 
                 def step(i, carry):
@@ -454,41 +484,103 @@
     for b in range(batches):
         for part in range(len(LAST)):
             for d in range(2):
-                last_copy(units - batches + b, d, part).wait_send()
-                out_copy(b, d, part).wait()
-
-
-def copy_kernel(src_ref, out_ref, held, in_sem, out_sem):
-    count = src_ref.shape[0] // COPY_ROWS
-
-    def move(src, dst, sem, i):
-        rows = pl.ds(i * COPY_ROWS, COPY_ROWS)
-        return pltpu.make_async_copy(src.at[rows, :], dst.at[rows, :], sem.at[i])
-
-    for i in range(count):
-        move(src_ref, held, in_sem, i).start()
-    for i in range(count):
-        move(src_ref, held, in_sem, i).wait()
-        move(held, out_ref, out_sem, i).start()
-    for i in range(count):
-        move(held, out_ref, out_sem, i).wait()
-
-
-def copy_out(mixed):
-    count = mixed.shape[0] // COPY_ROWS
+                if b == batches - 1 and part == len(LAST) - 1:
+                    for copy in tail_copies(d):
+                        copy.wait()
+                    last_copy(units - 1, d, part, True).wait_recv()
+                    last_copy(units - 1, d, part, True).wait_send()
+                else:
+                    last_copy(units - batches + b, d, part).wait_send()
+                    out_copy(b, d, part).wait()
+
+
+def copy_kernel(
+    groups,
+    mixed_ref,
+    tokens_ref,
+    own_ref,
+    sum_ref,
+    scale_ref,
+    out_ref,
+    held,
+    own,
+    sums,
+    scale,
+    in_sem,
+    tail_sem,
+    out_sem,
+):
+    rows, depth = mixed_ref.shape
+    first, size = LAST[-1]
+    start = rows - 2 * PIECE
+    tails = [start + d * PIECE + first for d in range(2)]
+    edges = [0] + [edge for tail in tails for edge in (tail, tail + size)] + [rows]
+    chunks = [
+        (at, min(COPY_ROWS, high - at))
+        for low, high in zip(edges[::2], edges[1::2])
+        for at in range(low, high, COPY_ROWS)
+    ]
+    blocks = [(mixed_ref, at, count) for at, count in chunks]
+    blocks += [(tokens_ref, at, size) for at in tails]
+
+    def fetch(i):
+        src, at, count = blocks[i]
+        span = pl.ds(at, count)
+        return pltpu.make_async_copy(src.at[span, :], held.at[span, :], in_sem.at[i])
+
+    def put(i):
+        _, at, count = blocks[i]
+        span = pl.ds(at, count)
+        return pltpu.make_async_copy(held.at[span, :], out_ref.at[span, :], out_sem.at[i])
+
+    extras = [
+        pltpu.make_async_copy(src, dst, tail_sem.at[i])
+        for i, (src, dst) in enumerate(((own_ref, own), (sum_ref, sums), (scale_ref, scale)))
+    ]
+    order = list(range(len(chunks), len(blocks))) + list(range(len(chunks)))
+    for copy in extras:
+        copy.start()
+    for i in order:
+        fetch(i).start()
+    for copy in extras:
+        copy.wait()
+    width = depth // groups
+    for d, at in enumerate(tails):
+        i = len(chunks) + d
+        fetch(i).wait()
+        for g in range(groups):
+            cols = slice(g * width, (g + 1) * width)
+            total = own[d, :, cols].astype(jnp.float32) + sums[d, :, cols].astype(jnp.float32)
+            held[at : at + size, cols] = (
+                held[at : at + size, cols].astype(jnp.float32) + total * scale[d, :, g : g + 1]
+            ).astype(jnp.bfloat16)
+        put(i).start()
+    for i in range(len(chunks)):
+        fetch(i).wait()
+        put(i).start()
+    for i in order:
+        put(i).wait()
+
+
+def copy_out(groups, mixed, tokens, own, sums, scale):
     any_spec = pl.BlockSpec(memory_space=pl.ANY)
+    count = mixed.shape[0] // COPY_ROWS + 6
     return pl.pallas_call(
-        copy_kernel,
-        in_specs=[any_spec],
+        functools.partial(copy_kernel, groups),
+        in_specs=[any_spec] * 5,
         out_specs=any_spec,
         out_shape=jax.ShapeDtypeStruct(mixed.shape, mixed.dtype),
         scratch_shapes=[
             pltpu.VMEM(mixed.shape, mixed.dtype),
+            pltpu.VMEM(own.shape, own.dtype),
+            pltpu.VMEM(sums.shape, sums.dtype),
+            pltpu.VMEM(scale.shape, scale.dtype),
             pltpu.SemaphoreType.DMA((count,)),
+            pltpu.SemaphoreType.DMA((3,)),
             pltpu.SemaphoreType.DMA((count,)),
         ],
         compiler_params=pltpu.CompilerParams(vmem_limit_bytes=56 * 1024 * 1024),
-    )(mixed)
+    )(mixed, tokens, own, sums, scale)
 
 
 def on_device(
@@ -509,11 +601,17 @@
     any_spec = pl.BlockSpec(memory_space=pl.ANY)
     bf16 = jnp.bfloat16
     dma = pltpu.SemaphoreType.DMA
-    mixed = pl.pallas_call(
+    tail = (2, LAST[-1][1])
+    mixed, own, sums, scale = pl.pallas_call(
         functools.partial(layer_kernel, ranks, batches),
         in_specs=[any_spec] * 11,
-        out_specs=any_spec,
-        out_shape=jax.ShapeDtypeStruct(tokens.shape, bf16),
+        out_specs=[any_spec] * 4,
+        out_shape=[
+            jax.ShapeDtypeStruct(tokens.shape, bf16),
+            jax.ShapeDtypeStruct(tail + (depth,), bf16),
+            jax.ShapeDtypeStruct(tail + (depth,), bf16),
+            jax.ShapeDtypeStruct(tail + (128,), jnp.float32),
+        ],
         scratch_shapes=[
             pltpu.VMEM((units + batches, unit, depth), bf16),
             pltpu.VMEM((units - batches, unit, depth), bf16),
@@ -541,6 +639,7 @@
             dma((2, kv_heads)),
             dma((batches, 2, len(FIRST))),
             dma((batches, 2, len(LAST))),
+            dma((2, 2)),
             dma((units - batches, 2)),
             dma((units - batches, 2)),
             dma((units - batches, 2)),
@@ -564,7 +663,7 @@
         sine_part,
         bias,
     )
-    return copy_out(mixed)
+    return copy_out(exponents.shape[1], mixed, tokens, own, sums, scale)
 
 
 def solution(mesh):

time: 178 us -> 179 us (level)
  no operation moved by 1% of the time
where the time goes in v4:
time: 179 us
  Pallas kernels  178 us (99%)
    pallas_call x1, Pallas kernels, on_device(): pl.pallas_call(functools.partial(layer_kernel, ranks, batches), in_specs=...  175 us
    pallas_call x1, Pallas kernels, copy_out(): pl.pallas_call(functools.partial(copy_kernel, groups), in_specs=[any_spec...  3.81 us

profile of v4, /device:TPU:0, one launch (start us, length us, event | category | flops | bytes accessed | tf_op | source)
XLA Modules:
  0.0 178.5 jit_solution(12489640056596463796)
XLA Ops:
  0.0 174.7 %shard_map.109 = (bf16[320,4096]{1,0:T(8,128)(2,1)}, bf16[2,16,4096]{2,1,0:T(8,128)(2,1)}, bf16[2,16,4096]{2,1,0:T(8,128)(2,1)}, f32[2,16,128]{2,1,0:T(8,128)}) custom-call(bf16[320,4096]{1,0:T(8,128)(2,1)} %tokens_ref.3, bf16[4096]{0:T(1024)(128)(2,1)} %gain_in.1, bf16[4096,2048]{1,0:T(8,128)(2,1)} %wq_ref.1, bf16[4096,256]{1,0:T(8,128)(2,1)} %wk_ref.1, ...), custom_call_target="tpu_custom_call" | custom-call | tf_op jit(solution)/shard_map/pallas_call | solution.py:605
  174.7 3.8 %shard_map.110 = bf16[320,4096]{1,0:T(8,128)(2,1)} custom-call(bf16[320,4096]{1,0:T(8,128)(2,1)} %get-tuple-element.9.mixed_ref, bf16[320,4096]{1,0:T(8,128)(2,1)} %tokens_ref.3, bf16[2,16,4096]{2,1,0:T(8,128)(2,1)} %get-tuple-element.10.own_ref, bf16[2,16,4096]{2,1,0:T(8,128)(2,1)} %get-tuple-element.11.sum_ref, f32[2,16,128]{2,1,0:T(8,128)} %get-tuple-element.12.scale_ref), custom_call_target="tpu_custom_call" | custom-call | tf_op jit(solution)/shard_map/pallas_call | solution.py:568
